TPU v7x, 32 devices: a whole 2x2x4 slice. The times are simulated.
32 devices in a mesh: dp: 8 (over z, core), tp: 4 (over y, x).
Axes of the slice: x: 2, y: 2, z: 4, core: 2. Of those that a mesh axis runs over, the one named last changes fastest.
Arguments:
- master: float32 [4096, 10240], P(('dp', 'tp')), may hold values from -0.09375 to 0.09375
- grad: float32 [4096, 10240], P(('dp', 'tp')), may hold values from -0.006 to 0.006
- exp_avg: float32 [4096, 10240], P(('dp', 'tp')), may hold values from -0.006 to 0.006
- exp_avg_sq: float32 [4096, 10240], P(('dp', 'tp')), may hold values from 1e-08 to 1e-05
Outputs:
- new_master: float32 [4096, 10240], P(('dp', 'tp'))
- new_avg: float32 [4096, 10240], P(('dp', 'tp'))
- new_avg_sq: float32 [4096, 10240], P(('dp', 'tp'))
- engine_qkv: bfloat16 [4096, 10240], P(None, 'tp')
All inputs are finite; a program needn't handle non-finite values.
Results may differ from a plain program's by a relative error of at most 0.001.
Values may be sent and summed in bfloat16 or wider, within the bound.
No kernel may reach another device: no remote copies, remote signals or barrier semaphores. Data moves between devices by JAX's collectives and lax.ppermute only.
A program may use at most 128 MiB of HBM per device.

v0:
```python
import jax
import jax.numpy as jnp
from jax import lax
from jax.sharding import PartitionSpec as P

QH = 64
KVH = 8
HS = 128


def joined_slices(weights, tp_count):
    rows = weights.shape[0]
    query = weights[:, : QH * HS].reshape(rows, tp_count, QH // tp_count * HS)
    keys = weights[:, QH * HS : (QH + KVH) * HS].reshape(rows, tp_count, KVH // tp_count * HS)
    values = weights[:, (QH + KVH) * HS :].reshape(rows, tp_count, KVH // tp_count * HS)
    return jnp.concatenate([query, keys, values], axis=2).reshape(rows, -1)


def body(master, grad, exp_avg, exp_avg_sq):
    corr_one = 1.0 - 0.9**10
    corr_two = 1.0 - 0.999**10
    new_avg = 0.9 * exp_avg + 0.1 * grad
    new_avg_sq = 0.999 * exp_avg_sq + 0.001 * grad * grad
    update = new_avg / corr_one / (jnp.sqrt(new_avg_sq / corr_two) + 1e-08)
    new_master = master - 0.001 * (update + 0.1 * master)
    tp_count = lax.axis_size("tp")
    ordered = joined_slices(new_master, tp_count).astype(jnp.bfloat16)
    group_rows = lax.all_to_all(ordered, "tp", split_axis=1, concat_axis=0, tiled=True)
    engine_qkv = lax.all_gather(group_rows, "dp", axis=0, tiled=True)
    return (new_master, new_avg, new_avg_sq, engine_qkv)


def solution(mesh):
    in_specs = (
        P(("dp", "tp"), None),
        P(("dp", "tp"), None),
        P(("dp", "tp"), None),
        P(("dp", "tp"), None),
    )
    out_specs = (P(("dp", "tp"), None), P(("dp", "tp"), None), P(("dp", "tp"), None), P(None, "tp"))
    return jax.shard_map(body, mesh=mesh, in_specs=in_specs, out_specs=out_specs, check_vma=False)
```

profile of v0, /device:TPU:0, one launch (start us, length us, event | category | flops | bytes accessed | tf_op | source)
XLA Modules:
  0.0 267.6 jit_solution(15748844206019149272)
XLA Ops:
  7.2 0.0 all-gather.2.cloned.1.call-start
  7.2 14.4 %fusion.1 = (bf16[128,10240]{1,0:T(8,128)(2,1)S(1)}, f32[128,10240]{1,0:T(8,128)}, f32[128,10240]{1,0:T(8,128)}, f32[128,10240]{1,0:T(8,128)}) fusion(f32[128,10240]{1,0:T(8,128)} %param.4, f32[128,10240]{1,0:T(8,128)} %param.5, f32[128,10240]{1,0:T(8,128)} %param.6, f32[128,10240]{1,0:T(8,128)} %param.7), kind=kLoop, calls=%fused_computation.8 | loop fusion | flops 20971520 | bytes 39321600 | tf_op jit(solution)/shard_map/convert.8
  21.6 0.1 slice.15
  21.8 0.1 copy.17
  22.0 0.2 pad_maximum_fusion
  22.2 36.1 %all_to_all.16 = bf16[128,4,2560]{2,0,1:T(8,128)(2,1)} all-to-all(bf16[128,4,2560]{2,0,1:T(8,128)(2,1)S(1)} %pad_maximum_fusion), channel_id=1, replica_groups=mesh['dp'=8,'tp'=4] {'tp'}, dimensions={1} | all-to-all | bytes 5242880 | tf_op jit(solution)/shard_map/all_to_all | solution.py:28
  58.3 0.0 all-gather.2.cloned.1.call-update
  58.3 185.3 %all-gather.2.cloned.1.call-done = bf16[4096,2560]{1,0:T(8,128)(2,1)} async-done(((bf16[512,2560]{1,0:T(8,128)(2,1)}), bf16[4096,2560]{1,0:T(8,128)(2,1)}) %all-gather.2.cloned.1.call-update) | async-done | bytes 20971536 | tf_op jit(solution)/shard_map/all_gather | solution.py:29
  243.6 17.1 %copy.19 = bf16[4096,2560]{1,0:T(8,128)(2,1)} copy(bf16[4096,2560]{1,0:T(8,128)(2,1)} %all-gather.2.cloned.1.call-done) | data formatting | bytes 41943040
  (2 shorter events, 0.1 us)
Async XLA Ops:
  7.2 236.5 %all-gather.2.cloned.1.call-start = ((), (), s32[]{:S(2)}) async-start(), calls=%async_computation.1 | async-start | bytes 23592960 | tf_op jit(solution)/shard_map/all_gather | solution.py:29
Sparse Core Ops, SparseCore 0:
  58.4 185.1 all-gather.1
where the time goes:
time: 268 us
  waiting for transfers between devices  185 us (69%)
  blocking collectives  36.1 us (13%)
  local copies, waits for them, and re-layouts  17.5 us (7%)
  other arithmetic  14.6 us (5%)
  between operations  14.1 us (5%)
    all_gather x1, waiting for transfers between devices, body(): engine_qkv = lax.all_gather(group_rows, 'dp', axis=0, tiled=True)  185 us
    all_to_all x1, blocking collectives, body(): lax.all_to_all(ordered, 'tp', split_axis=1, concat_axis=0, tiled=True)  36.1 us
    unnamed x1, local copies, waits for them, and re-layouts  17.1 us
    another operation x1, other arithmetic  14.4 us
  transfers between devices with their start and end apart: 1, of which 1 were waited for; matrix products, arithmetic and copies ran while one was open for 0% of the time, Pallas kernels for 0%

commit v1 on v0

v1 whole, which is shorter than its diff:
```python
import jax
import jax.numpy as jnp
from jax import lax
from jax.experimental import pallas as pl
from jax.experimental.pallas import tpu as pltpu
from jax.sharding import PartitionSpec as P

QH = 64
KVH = 8
HS = 128


def step(master, grad, exp_avg, exp_avg_sq):
    corr_one = 1.0 - 0.9**10
    corr_two = 1.0 - 0.999**10
    new_avg = 0.9 * exp_avg + 0.1 * grad
    new_avg_sq = 0.999 * exp_avg_sq + 0.001 * grad * grad
    update = new_avg / corr_one / (jnp.sqrt(new_avg_sq / corr_two) + 1e-08)
    new_master = master - 0.001 * (update + 0.1 * master)
    return new_master, new_avg, new_avg_sq


def slice_kernel(which, master, grad, avg, sq, piece):
    piece[...] = step(master[...], grad[...], avg[...], sq[...])[0].astype(jnp.bfloat16)


def step_slice(which, args, tp_count):
    rows = args[0].shape[0]
    width = KVH // tp_count * HS
    per_query = QH // KVH
    steps = per_query + 2

    def column(j, s):
        return (0, jnp.where(j < per_query, s[0] * per_query + j, j * tp_count + s[0]))

    return pl.pallas_call(
        slice_kernel,
        grid_spec=pltpu.PrefetchScalarGridSpec(
            num_scalar_prefetch=1,
            grid=(steps,),
            in_specs=[pl.BlockSpec((rows, width), column)] * 4,
            out_specs=pl.BlockSpec((rows, width), lambda j, s: (0, j)),
        ),
        out_shape=jax.ShapeDtypeStruct((rows, steps * width), jnp.bfloat16),
    )(which.reshape(1), *args)


def joined_slices(weights, tp_count):
    rows = weights.shape[0]
    query = weights[:, : QH * HS].reshape(rows, tp_count, QH // tp_count * HS)
    keys = weights[:, QH * HS : (QH + KVH) * HS].reshape(rows, tp_count, KVH // tp_count * HS)
    values = weights[:, (QH + KVH) * HS :].reshape(rows, tp_count, KVH // tp_count * HS)
    return jnp.concatenate([query, keys, values], axis=2)


def place(out, gathered, tp, first, last, tp_count, rows):
    width = gathered.shape[1]
    kinds = last - first
    count = gathered.shape[0] // rows
    filled = [] if out is None else [out]

    def kernel(tp_ref, src, *refs):
        dst, held, sem_in, sem_out = refs[-4:]

        def load(i):
            return pltpu.make_async_copy(src.at[pl.ds(i * rows, rows), :], held.at[i], sem_in.at[i])

        def store(i):
            block = (i // kinds) * tp_count + (tp_ref[0] ^ (first + i % kinds))
            start = pl.multiple_of(block * rows, rows)
            return pltpu.make_async_copy(held.at[i], dst.at[pl.ds(start, rows), :], sem_out.at[i])

        for i in range(count):
            load(i).start()
        for i in range(count):
            load(i).wait()
            store(i).start()
        for i in range(count):
            store(i).wait()

    total = gathered.shape[0] // kinds * tp_count
    return pl.pallas_call(
        kernel,
        in_specs=[pl.BlockSpec(memory_space=pltpu.SMEM)]
        + [pl.BlockSpec(memory_space=pl.ANY)] * (1 + len(filled)),
        out_specs=pl.BlockSpec(memory_space=pl.ANY),
        out_shape=jax.ShapeDtypeStruct((total, width), gathered.dtype),
        scratch_shapes=[
            pltpu.VMEM((count, rows, width), gathered.dtype),
            pltpu.SemaphoreType.DMA((count,)),
            pltpu.SemaphoreType.DMA((count,)),
        ],
        input_output_aliases={2: 0} if filled else {},
    )(tp.reshape(1), gathered, *filled)


def body(master, grad, exp_avg, exp_avg_sq):
    tp_count = lax.axis_size("tp")
    tp = lax.axis_index("tp").astype(jnp.int32)
    rows = master.shape[0]
    args = (master, grad, exp_avg, exp_avg_sq)
    own = step_slice(tp, args, tp_count)
    own_gathered = lax.all_gather(own, "dp", axis=0, tiled=True)
    *args, own = lax.optimization_barrier((*args, own))
    new_master, new_avg, new_avg_sq = step(*args)
    ordered = joined_slices(new_master.astype(jnp.bfloat16), tp_count)
    others = []
    for k in range(1, tp_count):
        piece = lax.dynamic_index_in_dim(ordered, tp ^ k, axis=1, keepdims=False)
        others.append(lax.ppermute(piece, "tp", [(i, i ^ k) for i in range(tp_count)]))
    gathered = lax.all_gather(jnp.concatenate(others, axis=0), "dp", axis=0, tiled=True)
    out = place(None, own_gathered, tp, 0, 1, tp_count, rows)
    out = place(out, gathered, tp, 1, tp_count, tp_count, rows)
    return (new_master, new_avg, new_avg_sq, out)


def solution(mesh):
    rows = P(("dp", "tp"), None)
    return jax.shard_map(
        body, mesh=mesh, in_specs=(rows,) * 4, out_specs=(rows, rows, rows, P(None, "tp")), check_vma=False
    )
```

time: 268 us -> 235 us (0.88)
  blocking collectives: 36.1 us -> 0 us
  Pallas kernels: 0 us -> 23.4 us
  local copies, waits for them, and re-layouts: 17.5 us -> 3.45 us
  waiting for transfers between devices: 185 us -> 173 us
  starting transfers between devices: 0.04 us -> 4.7 us
    all_gather x1 -> x2, waiting for transfers between devices: 185 us -> 143 us  [the longest x1 138 us: body(): lax.all_gather(jnp.concatenate(others, axis=0), 'dp', axis=0, tiled=True)]
    all_to_all x1 -> x0, blocking collectives: 36.1 us -> none  [body(): lax.all_to_all(ordered, 'tp', split_axis=1, concat_axis=0, tiled=True)]
    ppermute x0 -> x3, waiting for transfers between devices: none -> 29.9 us  [body(): lax.ppermute(piece, 'tp', [(i, i ^ k) for i in range(tp_count)])]
    pallas_call x0 -> x3, Pallas kernels: none -> 23.4 us  [the longest x2 16 us: place(): pl.pallas_call(kernel, in_specs=[pl.BlockSpec(memory_space=pltpu.SMEM)] +...]
    unnamed x1 -> x2, local copies, waits for them, and re-layouts: 17.1 us -> 1.79 us
    convert_element_type x0 -> x1, other arithmetic: none -> 14.4 us  [body(): ordered = joined_slices(new_master.astype(jnp.bfloat16), tp_count)]
    another operation x1 -> x0, other arithmetic: 14.4 us -> none
    ppermute x0 -> x3, starting transfers between devices: none -> 4.62 us  [body(): lax.ppermute(piece, 'tp', [(i, i ^ k) for i in range(tp_count)])]
  transfers between devices with their start and end apart: 1 -> 5, of which waited for: 1 -> 5; matrix products, arithmetic and copies ran while one was open for 0% -> 8% of each run, Pallas kernels for 0% -> 2%
where the time goes in v1:
time: 235 us
  waiting for transfers between devices  173 us (74%)
  Pallas kernels  23.4 us (10%)
  other arithmetic  15.8 us (7%)
  between operations  14.1 us (6%)
  starting transfers between devices  4.7 us (2%)
  local copies, waits for them, and re-layouts  3.45 us (1%)
    all_gather x1, waiting for transfers between devices, body(): lax.all_gather(jnp.concatenate(others, axis=0), 'dp', axis=0, tiled=True)  138 us
    ppermute x3, waiting for transfers between devices, body(): lax.ppermute(piece, 'tp', [(i, i ^ k) for i in range(tp_count)])  29.9 us
    pallas_call x2, Pallas kernels, place(): pl.pallas_call(kernel, in_specs=[pl.BlockSpec(memory_space=pltpu.SMEM)] +...  16 us
    convert_element_type x1, other arithmetic, body(): ordered = joined_slices(new_master.astype(jnp.bfloat16), tp_count)  14.4 us
    pallas_call x1, Pallas kernels, step_slice(): pl.pallas_call(slice_kernel, grid_spec=pltpu.PrefetchScalarGridSpec(num_s...  7.41 us
    all_gather x1, waiting for transfers between devices, body(): own_gathered = lax.all_gather(own, 'dp', axis=0, tiled=True)  4.95 us
  transfers between devices with their start and end apart: 5, of which 5 were waited for; matrix products, arithmetic and copies ran while one was open for 8% of the time, Pallas kernels for 2%

profile of v1, /device:TPU:0, one launch (start us, length us, event | category | flops | bytes accessed | tf_op | source)
XLA Modules:
  0.0 234.7 jit_solution(7771930531621242779)
XLA Ops:
  7.2 0.0 all-gather.5.cloned.1.call-start
  7.2 7.4 %shard_map.75 = bf16[128,2560]{1,0:T(8,128)(2,1)} custom-call(s32[1]{0:T(128)} %bitcast.which.tp_ref, f32[128,10240]{1,0:T(8,128)} %master.1, f32[128,10240]{1,0:T(8,128)} %grad.1, f32[128,10240]{1,0:T(8,128)} %avg.1, f32[128,10240]{1,0:T(8,128)} %sq.1), custom_call_target="tpu_custom_call" | custom-call | tf_op jit(solution)/shard_map/pallas_call | solution.py:36
  14.6 0.0 all-gather.5.cloned.1.call-update
  14.6 0.0 all-gather.3.cloned.1.call-start
  14.7 14.4 %fusion.1 = (bf16[128,10240]{1,0:T(8,128)(2,1)S(1)}, f32[128,10240]{1,0:T(8,128)}, f32[128,10240]{1,0:T(8,128)}, f32[128,10240]{1,0:T(8,128)}) fusion(f32[128,10240]{1,0:T(8,128)} %master.1, f32[128,10240]{1,0:T(8,128)} %grad.1, f32[128,10240]{1,0:T(8,128)} %avg.1, f32[128,10240]{1,0:T(8,128)} %sq.1), kind=kLoop, calls=%fused_computation.11 | loop fusion | flops 20971520 | bytes 39321600 | tf_op jit(solution)/shard_map/convert_element_type | solution.py:106
  29.1 1.5 slice.12
  30.6 1.8 bitcast_dynamic-update-slice_fusion
  32.5 0.2 dynamic-slice_bitcast_fusion.2
  32.6 3.1 %collective-permute-start = (bf16[128,2560]{1,0:T(8,128)(2,1)S(1)}, bf16[128,2560]{1,0:T(8,128)(2,1)S(1)}, u32[]{:S(2)}, u32[]{:S(2)}) collective-permute-start(bf16[128,2560]{1,0:T(8,128)(2,1)S(1)} %get-tuple-element.16), channel_id=1, source_target_pairs={{0,1},{1,0},{2,3},{3,2},{4,5},{5,4},{6,7},{7,6},{8,9},{9,8},{10,11... | collective-permute-start | bytes 1966088 | tf_op jit(solution)/shard_map/ppermute | solution.py:110
  35.7 1.5 collective-permute-start.2
  37.2 0.1 collective-permute-start.1
  37.2 14.0 %collective-permute-done = bf16[128,2560]{1,0:T(8,128)(2,1)S(1)} collective-permute-done((bf16[128,2560]{1,0:T(8,128)(2,1)S(1)}, bf16[128,2560]{1,0:T(8,128)(2,1)S(1)}, u32[]{:S(2)}, u32[]{:S(2)}) %collective-permute-start) | collective-permute-done | bytes 655392 | tf_op jit(solution)/shard_map/ppermute | solution.py:110
  51.3 14.5 %collective-permute-done.2 = bf16[128,2560]{1,0:T(8,128)(2,1)S(1)} collective-permute-done((bf16[128,2560]{1,0:T(8,128)(2,1)S(1)}, bf16[128,2560]{1,0:T(8,128)(2,1)S(1)}, u32[]{:S(2)}, u32[]{:S(2)}) %collective-permute-start.2) | collective-permute-done | bytes 655392 | tf_op jit(solution)/shard_map/ppermute | solution.py:110
  65.8 1.4 collective-permute-done.1
  67.1 1.4 pad_maximum_fusion
  68.5 0.0 all-gather.3.cloned.1.call-update
  68.6 5.0 %all-gather.5.cloned.1.call-done.src = bf16[1024,2560]{1,0:T(8,128)(2,1)} async-done(((bf16[128,2560]{1,0:T(8,128)(2,1)}), bf16[1024,2560]{1,0:T(8,128)(2,1)}) %all-gather.5.cloned.1.call-update) | async-done | bytes 5242896 | tf_op jit(solution)/shard_map/all_gather | solution.py:103
  73.5 4.6 %shard_map.76.refs_0_ = bf16[4096,2560]{1,0:T(8,128)(2,1)} custom-call(s32[1]{0:T(128)} %bitcast.which.tp_ref, bf16[1024,2560]{1,0:T(8,128)(2,1)} %all-gather.5.cloned.1.call-done.src), custom_call_target="tpu_custom_call" | custom-call | tf_op jit(solution)/shard_map/pallas_call | solution.py:82
  78.1 138.3 %all-gather.3.cloned.1.call-done.src = bf16[3072,2560]{1,0:T(8,128)(2,1)} async-done(((bf16[384,2560]{1,0:T(8,128)(2,1)}), bf16[3072,2560]{1,0:T(8,128)(2,1)}) %all-gather.3.cloned.1.call-update) | async-done | bytes 15728656 | tf_op jit(solution)/shard_map/all_gather | solution.py:111
  216.4 11.4 %shard_map.77 = bf16[4096,2560]{1,0:T(8,128)(2,1)} custom-call(s32[1]{0:T(128)} %bitcast.which.tp_ref, bf16[3072,2560]{1,0:T(8,128)(2,1)} %all-gather.3.cloned.1.call-done.src, bf16[4096,2560]{1,0:T(8,128)(2,1)} %shard_map.76.refs_0_), custom_call_target="tpu_custom_call", output_to_operand_aliasing={{}: (2, {})} | custom-call | tf_op jit(solution)/shard_map/pallas_call | solution.py:82
  (3 shorter events, 0.1 us)
Async XLA Ops:
  7.2 66.3 %all-gather.5.cloned.1.call-start = ((), (), s32[]{:S(2)}) async-start(), calls=%async_computation.1 | async-start | bytes 5898240 | tf_op jit(solution)/shard_map/all_gather | solution.py:103
  14.6 201.8 %all-gather.3.cloned.1.call-start = ((), (), s32[]{:S(2)}) async-start(), calls=%async_computation | async-start | bytes 17694720 | tf_op jit(solution)/shard_map/all_gather | solution.py:111
  32.6 18.7 %collective-permute-start = (bf16[128,2560]{1,0:T(8,128)(2,1)S(1)}, bf16[128,2560]{1,0:T(8,128)(2,1)S(1)}, u32[]{:S(2)}, u32[]{:S(2)}) collective-permute-start(bf16[128,2560]{1,0:T(8,128)(2,1)S(1)} %get-tuple-element.16), channel_id=1, source_target_pairs={{0,1},{1,0},{2,3},{3,2},{4,5},{5,4},{6,7},{7,6},{8,9},{9,8},{10,11... | collective-permute-start | bytes 1966088 | tf_op jit(solution)/shard_map/ppermute | solution.py:110
  35.7 30.1 %collective-permute-start.2 = (bf16[128,2560]{1,0:T(8,128)(2,1)S(1)}, bf16[128,2560]{1,0:T(8,128)(2,1)S(1)}, u32[]{:S(2)}, u32[]{:S(2)}) collective-permute-start(bf16[128,2560]{1,0:T(8,128)(2,1)S(1)} %get-tuple-element.17), channel_id=1, source_target_pairs={{0,3},{1,2},{2,1},{3,0},{4,7},{5,6},{6,5},{7,4},{8,11},{9,10},{10,... | collective-permute-start | bytes 1966088 | tf_op jit(solution)/shard_map/ppermute | solution.py:110
  37.2 30.0 %collective-permute-start.1 = (bf16[128,2560]{1,0:T(8,128)(2,1)S(1)}, bf16[128,2560]{1,0:T(8,128)(2,1)S(1)}, u32[]{:S(2)}, u32[]{:S(2)}) collective-permute-start(bf16[128,2560]{1,0:T(8,128)(2,1)S(1)} %get-tuple-element.18), channel_id=1, source_target_pairs={{0,2},{1,3},{2,0},{3,1},{4,6},{5,7},{6,4},{7,5},{8,10},{9,11},{10,... | collective-permute-start | bytes 1966088 | tf_op jit(solution)/shard_map/ppermute | solution.py:110
Sparse Core Ops, SparseCore 0:
  14.8 58.6 all-gather.4
  75.1 141.2 all-gather.2
